TPU v7x, 32 devices: a whole 2x2x4 slice. The times are simulated.
32 devices in a mesh: graph: 8 (over z, x), batch: 4 (over y, core).
Axes of the slice: x: 2, y: 2, z: 4, core: 2. Of those that a mesh axis runs over, the one named last changes fastest.
Arguments:
- node_latent: bfloat16 [4, 1024, 512], P('batch', 'graph'), may hold values from -6 to 6
- edge_latent: bfloat16 [4, 8192, 512], P('batch', 'graph'), may hold values from -6 to 6
- node_cotangent: bfloat16 [4, 1024, 512], P('batch', 'graph'), may hold values from -6 to 6
- edge_w_in: bfloat16 [2, 1536, 512], replicated, may hold values from -0.15625 to 0.15625
- edge_w_out: bfloat16 [2, 512, 512], replicated, may hold values from -0.25 to 0.25
- node_w_in: bfloat16 [2, 1024, 512], replicated, may hold values from -0.1875 to 0.1875
- node_w_out: bfloat16 [2, 512, 512], replicated, may hold values from -0.25 to 0.25
- edge_gain: float32 [2, 512], replicated, may hold values from 0.25 to 1.75
- node_gain: float32 [2, 512], replicated, may hold values from 0.25 to 1.75
- edge_slot: int32 [8192], P('graph'), may hold values from 0 to 383, as said below
- edge_receiver: int32 [8192], P('graph'), may hold values from 0 to 127
- send_list: int32 [64, 32], P('graph'), may hold values from 0 to 127, as said below
- edge_count: int32 [8], P('graph'), may hold values from 256 to 1024, as said below
Outputs:
- node_out: float32 [4, 1024, 512], P('batch', 'graph')
- node_grad: float32 [4, 1024, 512], P('batch', 'graph')
- grad_edge_in: float32 [2, 1536, 512], P(None, ('graph', 'batch'))
- grad_edge_out: float32 [2, 512, 512], P(None, ('graph', 'batch'))
- grad_node_in: float32 [2, 1024, 512], P(None, ('graph', 'batch'))
- grad_node_out: float32 [2, 512, 512], P(None, ('graph', 'batch'))
- grad_edge_gain: float32 [2, 512], P(None, ('graph', 'batch'))
- grad_node_gain: float32 [2, 512], P(None, ('graph', 'batch'))
Inputs may be any that keep to these rules, and one draw needn't show every extreme that they name: `edge_slot`: for edge j of partition p = j // 1024: a slot below 128 names a node of partition p; a slot s of 128 or more names row (s - 128) % 32 of the list that partition q = (s - 128) // 32 keeps for partition p, and q differs from p cyclically by 1 to 2 steps or by exactly 8 // 2 steps. `edge_receiver`: the receiving node is a node of the edge's own partition. `send_list`: row q * 8 + p holds 32 distinct node numbers within partition q, the nodes whose latents partition p may read. `edge_count`: edge slots at or above a partition's count carry no edge.
All inputs are finite; a program needn't handle non-finite values.
Results may differ from a plain program's by a relative error of at most 0.035.
Values may be sent and summed in bfloat16 or wider, within the bound.
A program may use at most 128 MiB of HBM per device.

v0:
```python
import jax
import jax.numpy as jnp
from jax import lax
from jax.sharding import PartitionSpec as P

EPSILON = 1e-05


def mlp_forward(pieces, weights, w_out, gain, live):
    pre_act = None
    for piece, weight in zip(pieces, weights):
        term = jnp.dot(piece, weight, preferred_element_type=jnp.float32)
        pre_act = term if pre_act is None else pre_act + term
    hidden = (pre_act * jax.nn.sigmoid(pre_act)).astype(jnp.bfloat16)
    projected = jnp.dot(hidden, w_out, preferred_element_type=jnp.float32)
    centre = projected - jnp.mean(projected, axis=-1, keepdims=True)
    inv_std = lax.rsqrt(jnp.mean(centre * centre, axis=-1, keepdims=True) + EPSILON)
    normed = centre * inv_std
    result = normed * gain
    if live is not None:
        result = result * live[:, None]
    return (result, (pre_act, hidden, normed, inv_std))


def mlp_backward(grad_out, pieces, weights, w_out, gain, live, saved):
    pre_act, hidden, normed, inv_std = saved
    if live is not None:
        grad_out = grad_out * live[:, None]
    grad_gain = jnp.sum(grad_out * normed, axis=0)
    grad_norm = grad_out * gain
    grad_proj = inv_std * (
        grad_norm
        - jnp.mean(grad_norm, axis=-1, keepdims=True)
        - normed * jnp.mean(grad_norm * normed, axis=-1, keepdims=True)
    )
    grad_proj_bf = grad_proj.astype(jnp.bfloat16)
    grad_w_out = jnp.dot(hidden.T, grad_proj_bf, preferred_element_type=jnp.float32)
    grad_hidden = jnp.dot(grad_proj_bf, w_out.T, preferred_element_type=jnp.float32)
    sigma = jax.nn.sigmoid(pre_act)
    grad_pre = grad_hidden * sigma * (1.0 + pre_act * (1.0 - sigma))
    grad_pre_bf = grad_pre.astype(jnp.bfloat16)
    grad_weights = [
        jnp.dot(piece.T, grad_pre_bf, preferred_element_type=jnp.float32) for piece in pieces
    ]
    grad_pieces = [
        jnp.dot(grad_pre_bf, weight.T, preferred_element_type=jnp.float32) for weight in weights
    ]
    return (grad_pieces, grad_weights, grad_w_out, grad_gain)


def reduce_terms(terms):
    partial_sum = (
        lax.psum_scatter(
            terms[0].astype(jnp.bfloat16), "graph", scatter_dimension=0, tiled=True
        ).astype(jnp.float32),
        lax.psum_scatter(
            terms[1].astype(jnp.bfloat16), "graph", scatter_dimension=0, tiled=True
        ).astype(jnp.float32),
        lax.psum_scatter(
            terms[2].astype(jnp.bfloat16), "graph", scatter_dimension=0, tiled=True
        ).astype(jnp.float32),
        lax.psum_scatter(
            terms[3].astype(jnp.bfloat16), "graph", scatter_dimension=0, tiled=True
        ).astype(jnp.float32),
        lax.psum_scatter(
            terms[4].astype(jnp.bfloat16), "graph", scatter_dimension=0, tiled=True
        ).astype(jnp.float32),
        lax.psum_scatter(
            terms[5].astype(jnp.bfloat16), "graph", scatter_dimension=0, tiled=True
        ).astype(jnp.float32),
    )
    return (
        lax.psum_scatter(
            partial_sum[0].astype(jnp.bfloat16), "batch", scatter_dimension=0, tiled=True
        ).astype(jnp.float32),
        lax.psum_scatter(
            partial_sum[1].astype(jnp.bfloat16), "batch", scatter_dimension=0, tiled=True
        ).astype(jnp.float32),
        lax.psum_scatter(
            partial_sum[2].astype(jnp.bfloat16), "batch", scatter_dimension=0, tiled=True
        ).astype(jnp.float32),
        lax.psum_scatter(
            partial_sum[3].astype(jnp.bfloat16), "batch", scatter_dimension=0, tiled=True
        ).astype(jnp.float32),
        lax.psum_scatter(
            partial_sum[4].astype(jnp.bfloat16), "batch", scatter_dimension=0, tiled=True
        ).astype(jnp.float32),
        lax.psum_scatter(
            partial_sum[5].astype(jnp.bfloat16), "batch", scatter_dimension=0, tiled=True
        ).astype(jnp.float32),
    )


def body(
    node_latent,
    edge_latent,
    node_cotangent,
    edge_w_in,
    edge_w_out,
    node_w_in,
    node_w_out,
    edge_gain,
    node_gain,
    edge_slot,
    edge_receiver,
    send_list,
    edge_count,
):
    width = node_latent.shape[2]
    node_rows = node_latent.shape[1]
    slot_count = edge_slot.shape[0]
    peer_rows = send_list.shape[1]
    layer_count = edge_w_in.shape[0]
    group_count = lax.axis_size("graph")
    live = (jnp.arange(slot_count, dtype=jnp.int32) < edge_count[0]).astype(jnp.float32)
    buffer_rows = node_rows + group_count * peer_rows
    state = node_latent[0].astype(jnp.float32)
    edge_state = edge_latent[0].astype(jnp.float32)
    edge_bf = edge_latent[0]
    records = []
    for layer in range(layer_count):
        node_bf = state.astype(jnp.bfloat16)
        if layer > 0:
            edge_bf = edge_state.astype(jnp.bfloat16)
        at_receiver = node_bf[edge_receiver]
        fetch_outgoing = node_bf[send_list]
        fetch_arrived = lax.all_to_all(
            fetch_outgoing, "graph", split_axis=0, concat_axis=0, tiled=True
        )
        sender_buffer = jnp.concatenate([node_bf, fetch_arrived.reshape(-1, width)], axis=0)
        from_sender = sender_buffer[edge_slot]
        w_first = edge_w_in[layer]
        edge_weights = [w_first[:width], w_first[2 * width :], w_first[width : 2 * width]]
        edge_inputs = [edge_bf, at_receiver, from_sender]
        message, edge_saved = mlp_forward(
            edge_inputs, edge_weights, edge_w_out[layer], edge_gain[layer], live
        )
        summed = jax.ops.segment_sum(message, edge_receiver, num_segments=node_rows).astype(
            jnp.bfloat16
        )
        n_first = node_w_in[layer]
        node_weights = [n_first[:width], n_first[width:]]
        node_inputs = [node_bf, summed]
        update, node_saved = mlp_forward(
            node_inputs, node_weights, node_w_out[layer], node_gain[layer], None
        )
        records.append(
            (edge_inputs, edge_weights, edge_saved, node_inputs, node_weights, node_saved)
        )
        edge_state = edge_state + message
        state = state + update
    grad_state = node_cotangent[0].astype(jnp.float32)
    grad_edge = None
    reduced = []
    for layer in reversed(range(layer_count)):
        edge_inputs, edge_weights, edge_saved, node_inputs, node_weights, node_saved = records[
            layer
        ]
        node_parts, node_wgrads, grad_n_out, grad_n_gain = mlp_backward(
            grad_state,
            node_inputs,
            node_weights,
            node_w_out[layer],
            node_gain[layer],
            None,
            node_saved,
        )
        grad_message = node_parts[1][edge_receiver]
        if grad_edge is not None:
            grad_message = grad_message + grad_edge
        edge_parts, edge_wgrads, grad_e_out, grad_e_gain = mlp_backward(
            grad_message,
            edge_inputs,
            edge_weights,
            edge_w_out[layer],
            edge_gain[layer],
            live,
            edge_saved,
        )
        grad_edge = edge_parts[0] if grad_edge is None else edge_parts[0] + grad_edge
        sender_grads = jax.ops.segment_sum(edge_parts[2], edge_slot, num_segments=buffer_rows)
        grad_state = (
            grad_state
            + node_parts[0]
            + jax.ops.segment_sum(edge_parts[1], edge_receiver, num_segments=node_rows)
        )
        return_grad_state = grad_state
        return_grad_state = return_grad_state + sender_grads[:node_rows]
        outgoing = sender_grads[node_rows:].reshape(group_count, peer_rows, width)
        arrived = lax.all_to_all(
            outgoing.astype(jnp.bfloat16), "graph", split_axis=0, concat_axis=0, tiled=True
        ).astype(outgoing.dtype)
        grad_state = return_grad_state.at[send_list.reshape(-1)].add(arrived.reshape(-1, width))
        grad_e_in = jnp.concatenate([edge_wgrads[0], edge_wgrads[2], edge_wgrads[1]], axis=0)
        grad_n_in = jnp.concatenate([node_wgrads[0], node_wgrads[1]], axis=0)
        reduced.append(
            reduce_terms((grad_e_in, grad_e_out, grad_n_in, grad_n_out, grad_e_gain, grad_n_gain))
        )
    reduced = reduced[::-1]
    stacked = tuple((jnp.stack([entry[index] for entry in reduced]) for index in range(6)))
    return (
        state[None],
        grad_state[None],
        stacked[0],
        stacked[1],
        stacked[2],
        stacked[3],
        stacked[4],
        stacked[5],
    )


def solution(mesh):
    in_specs = (
        P("batch", "graph", None),
        P("batch", "graph", None),
        P("batch", "graph", None),
        P(),
        P(),
        P(),
        P(),
        P(),
        P(),
        P("graph"),
        P("graph"),
        P("graph", None),
        P("graph"),
    )
    out_specs = (
        P("batch", "graph", None),
        P("batch", "graph", None),
        P(None, ("graph", "batch"), None),
        P(None, ("graph", "batch"), None),
        P(None, ("graph", "batch"), None),
        P(None, ("graph", "batch"), None),
        P(None, ("graph", "batch")),
        P(None, ("graph", "batch")),
    )
    return jax.shard_map(body, mesh=mesh, in_specs=in_specs, out_specs=out_specs, check_vma=False)
```

profile of v0, /device:TPU:0, one launch (start us, length us, event | category | flops | bytes accessed | tf_op | source)
XLA Modules:
  0.0 821.8 jit_solution(370736109194512029)
XLA Ops:
  8.1 2.8 gather_fusion.1
  10.9 7.3 all-to-all-start
  20.8 2.1 fusion.10
  23.4 2.3 copy.29
  26.4 5.1 gather_fusion
  31.4 3.4 fusion.52
  34.9 5.1 gather_fusion.2
  39.9 2.9 add_add_fusion.1
  45.8 1.9 copy.30
  47.6 7.3 scatter_custom_fusion
  56.4 1.5 fusion.116
  58.2 1.9 gather_fusion.4
  60.1 5.1 gather_fusion.3
  65.1 6.0 all-to-all-start.1
  71.6 3.5 fusion.30
  76.4 3.1 fusion.33
  79.7 5.1 gather_fusion.5
  84.7 3.5 add_add_fusion
  90.9 1.7 multiply_multiply_fusion
  92.6 2.9 copy.31
  95.5 7.5 scatter_custom_fusion.1
  109.7 4.9 gather_fusion.6
  114.7 3.0 copy.32
  117.7 3.7 multiply_reduce_fusion
  125.6 3.1 fusion.25
  128.8 8.2 scatter_custom_fusion.2
  136.9 1.8 slice.285
  138.7 5.9 all-to-all-start.2
  146.1 3.5 fusion.28
  149.5 7.4 scatter_fusion
  156.9 2.9 scatter_custom_fusion.4
  161.3 1.6 multiply_convert_fusion.6
  163.5 2.1 convolution_convert_fusion.2
  165.7 3.5 convolution_convert_fusion.7
  172.1 4.9 gather_fusion.7
  177.0 2.9 copy.33
  180.0 4.7 multiply_reduce_fusion.1
  186.3 1.6 convolution_convert_fusion.8
  192.7 2.0 convolution_convert_fusion.9
  198.5 3.0 multiply_convert_fusion
  207.3 30.7 %reduce-scatter.41.cloned.1.call-done = bf16[64,512]{1,0:T(8,128)(2,1)} async-done(((bf16[512,512]{1,0:T(8,128)(2,1)}), bf16[64,512]{1,0:T(8,128)(2,1)}) %reduce-scatter.41.cloned.1.call-update) | async-done | bytes 65552 | tf_op jit(solution)/shard_map/reduce_scatter | solution.py:62
  238.1 65.1 %reduce-scatter.29.cloned.1.call-done = bf16[64,512]{1,0:T(8,128)(2,1)} async-done(((bf16[512,512]{1,0:T(8,128)(2,1)}), bf16[64,512]{1,0:T(8,128)(2,1)}) %reduce-scatter.29.cloned.1.call-update) | async-done | bytes 65552 | tf_op jit(solution)/shard_map/reduce_scatter | solution.py:56
  305.8 19.7 %all-reduce.8 = (bf16[512]{0:T(512)(128)(2,1)S(1)}, bf16[512]{0:T(512)(128)(2,1)S(1)}, bf16[512]{0:T(512)(128)(2,1)S(1)}, bf16[512]{0:T(512)(128)(2,1)S(1)}) all-reduce(bf16[512]{0:T(512)(128)(2,1)S(1)} %copy-done.49, bf16[512]{0:T(512)(128)(2,1)S(1)} %copy-done.51, ...), channel_id=20, replica_groups=mesh['graph'=8,'batch'=4] {'graph'}, use_global_device_ids=true, to_apply=%region_44.0.clone | all-reduce | flops 2048 | bytes 8192
  325.7 5.6 all-reduce.9
  331.4 36.7 %reduce-scatter.25.cloned.1.call-done = bf16[64,512]{1,0:T(8,128)(2,1)} async-done(((bf16[512,512]{1,0:T(8,128)(2,1)}), bf16[64,512]{1,0:T(8,128)(2,1)}) %reduce-scatter.25.cloned.1.call-update) | async-done | bytes 65552 | tf_op jit(solution)/shard_map/reduce_scatter | solution.py:56
  368.9 65.7 %reduce-scatter.37.cloned.1.call-done = bf16[128,512]{1,0:T(8,128)(2,1)} async-done(((bf16[1024,512]{1,0:T(8,128)(2,1)}), bf16[128,512]{1,0:T(8,128)(2,1)}) %reduce-scatter.37.cloned.1.call-update) | async-done | bytes 131088 | tf_op jit(solution)/shard_map/reduce_scatter | solution.py:59
  434.6 3.1 fusion.47
  437.7 63.2 %reduce-scatter.33.cloned.1.call-done = bf16[128,512]{1,0:T(8,128)(2,1)} async-done(((bf16[1024,512]{1,0:T(8,128)(2,1)}), bf16[128,512]{1,0:T(8,128)(2,1)}) %reduce-scatter.33.cloned.1.call-update) | async-done | bytes 131088 | tf_op jit(solution)/shard_map/reduce_scatter | solution.py:59
  501.1 7.4 scatter_custom_fusion.5
  509.2 3.6 all-to-all-start.3
  514.2 56.5 %reduce-scatter.21.cloned.1.call-done = bf16[192,512]{1,0:T(8,128)(2,1)} async-done(((bf16[1536,512]{1,0:T(8,128)(2,1)}), bf16[192,512]{1,0:T(8,128)(2,1)}) %reduce-scatter.21.cloned.1.call-update) | async-done | bytes 196624 | tf_op jit(solution)/shard_map/reduce_scatter | solution.py:53
  570.9 2.1 fusion.50
  573.0 65.5 %reduce-scatter.17.cloned.1.call-done = bf16[192,512]{1,0:T(8,128)(2,1)} async-done(((bf16[1536,512]{1,0:T(8,128)(2,1)}), bf16[192,512]{1,0:T(8,128)(2,1)}) %reduce-scatter.17.cloned.1.call-update) | async-done | bytes 196624 | tf_op jit(solution)/shard_map/reduce_scatter | solution.py:53
  639.1 6.7 scatter_fusion.1
  645.8 2.4 scatter_custom_fusion.7
  648.2 11.1 %reduce-scatter.47.cloned.1.call-done = bf16[16,512]{1,0:T(8,128)(2,1)} async-done(((bf16[64,512]{1,0:T(8,128)(2,1)}), bf16[16,512]{1,0:T(8,128)(2,1)}) %reduce-scatter.47.cloned.1.call-update) | async-done | bytes 16400 | tf_op jit(solution)/shard_map/reduce_scatter | solution.py:82
  659.3 21.8 %reduce-scatter.43.cloned.1.call-done = bf16[16,512]{1,0:T(8,128)(2,1)} async-done(((bf16[64,512]{1,0:T(8,128)(2,1)}), bf16[16,512]{1,0:T(8,128)(2,1)}) %reduce-scatter.43.cloned.1.call-update) | async-done | bytes 16400 | tf_op jit(solution)/shard_map/reduce_scatter | solution.py:82
  682.5 20.6 %reduce-scatter.31.cloned.1.call-done = bf16[16,512]{1,0:T(8,128)(2,1)} async-done(((bf16[64,512]{1,0:T(8,128)(2,1)}), bf16[16,512]{1,0:T(8,128)(2,1)}) %reduce-scatter.31.cloned.1.call-update) | async-done | bytes 16400 | tf_op jit(solution)/shard_map/reduce_scatter | solution.py:76
  703.1 21.9 %reduce-scatter.27.cloned.1.call-done = bf16[16,512]{1,0:T(8,128)(2,1)} async-done(((bf16[64,512]{1,0:T(8,128)(2,1)}), bf16[16,512]{1,0:T(8,128)(2,1)}) %reduce-scatter.27.cloned.1.call-update) | async-done | bytes 16400 | tf_op jit(solution)/shard_map/reduce_scatter | solution.py:76
  726.3 20.7 %reduce-scatter.39.cloned.1.call-done = bf16[32,512]{1,0:T(8,128)(2,1)} async-done(((bf16[128,512]{1,0:T(8,128)(2,1)}), bf16[32,512]{1,0:T(8,128)(2,1)}) %reduce-scatter.39.cloned.1.call-update) | async-done | bytes 32784 | tf_op jit(solution)/shard_map/reduce_scatter | solution.py:79
  747.1 22.0 %reduce-scatter.35.cloned.1.call-done = bf16[32,512]{1,0:T(8,128)(2,1)} async-done(((bf16[128,512]{1,0:T(8,128)(2,1)}), bf16[32,512]{1,0:T(8,128)(2,1)}) %reduce-scatter.35.cloned.1.call-update) | async-done | bytes 32784 | tf_op jit(solution)/shard_map/reduce_scatter | solution.py:79
  770.5 20.7 %reduce-scatter.23.cloned.1.call-done = bf16[48,512]{1,0:T(8,128)(2,1)} async-done(((bf16[192,512]{1,0:T(8,128)(2,1)}), bf16[48,512]{1,0:T(8,128)(2,1)}) %reduce-scatter.23.cloned.1.call-update) | async-done | bytes 49168 | tf_op jit(solution)/shard_map/reduce_scatter | solution.py:73
  791.1 22.1 %reduce-scatter.19.cloned.1.call-done = bf16[48,512]{1,0:T(8,128)(2,1)} async-done(((bf16[192,512]{1,0:T(8,128)(2,1)}), bf16[48,512]{1,0:T(8,128)(2,1)}) %reduce-scatter.19.cloned.1.call-update) | async-done | bytes 49168 | tf_op jit(solution)/shard_map/reduce_scatter | solution.py:73
  813.3 1.5 maximum_convert_fusion
  (242 shorter events, 55.7 us)
Async XLA Ops:
  7.2 11.0 %copy-start.44 = (s32[8,32]{1,0:T(8,128)S(1)}, s32[8,32]{1,0:T(8,128)}, u32[]{:S(2)}) copy-start(s32[8,32]{1,0:T(8,128)} %param.24) | copy-start | bytes 3076
  7.2 12.3 %copy-start.1 = (bf16[1,128,512]{2,1,0:T(8,128)(2,1)S(1)}, bf16[1,128,512]{2,1,0:T(8,128)(2,1)}, u32[]{:S(2)}) copy-start(bf16[1,128,512]{2,1,0:T(8,128)(2,1)} %param.13) | copy-start | bytes 393220
  7.2 11.1 %copy-start.36 = (s32[1024]{0:T(1024)S(1)}, s32[1024]{0:T(1024)}, u32[]{:S(2)}) copy-start(s32[1024]{0:T(1024)} %param.23) | copy-start | bytes 12292
  7.2 11.1 %copy-start.54 = (s32[1024]{0:T(1024)S(1)}, s32[1024]{0:T(1024)}, u32[]{:S(2)}) copy-start(s32[1024]{0:T(1024)} %param.22) | copy-start | bytes 12292
  7.2 11.1 %copy-start.52 = (f32[2,512]{1,0:T(2,128)S(1)}, f32[2,512]{1,0:T(2,128)}, u32[]{:S(2)}) copy-start(f32[2,512]{1,0:T(2,128)} %param.20) | copy-start | bytes 12292
  7.2 11.7 %copy-start.53 = (f32[2,512]{1,0:T(2,128)S(1)}, f32[2,512]{1,0:T(2,128)}, u32[]{:S(2)}) copy-start(f32[2,512]{1,0:T(2,128)} %param.21) | copy-start | bytes 12292
  10.9 23.9 %all-to-all-start = ((bf16[8,32,512]{2,1,0:T(8,128)(2,1)}), bf16[8,32,512]{2,1,0:T(8,128)(2,1)S(1)}, u32[]{:S(2)}, u32[]{:S(2)}) async-start(bf16[8,32,512]{2,1,0:T(8,128)(2,1)} %bitcast.5), calls=%async_computation | async-start | bytes 524288 | tf_op jit(solution)/shard_map/all_to_all | solution.py:127
  18.9 25.6 %copy-start.40 = (f32[1,512]{1,0:T(1,128)}, f32[1,512]{1,0:T(1,128)S(1)}, u32[]{:S(2)}) copy-start(f32[1,512]{1,0:T(1,128)S(1)} %get-tuple-element.33) | copy-start | bytes 6148
  19.5 38.6 %copy-start.42 = (f32[1,512]{1,0:T(1,128)}, f32[1,512]{1,0:T(1,128)S(1)}, u32[]{:S(2)}) copy-start(f32[1,512]{1,0:T(1,128)S(1)} %get-tuple-element.31) | copy-start | bytes 6148
  39.9 2.9 copy-start.57
  55.0 5.1 copy-start.16
  57.8 7.3 copy-start.45
  58.0 7.1 copy-start.47
  65.1 14.5 %all-to-all-start.1 = ((bf16[8,32,512]{2,1,0:T(8,128)(2,1)}), bf16[8,32,512]{2,1,0:T(8,128)(2,1)S(1)}, u32[]{:S(2)}, u32[]{:S(2)}) async-start(bf16[8,32,512]{2,1,0:T(8,128)(2,1)} %bitcast.17), calls=%async_computation.1 | async-start | bytes 524288 | tf_op jit(solution)/shard_map/all_to_all | solution.py:127
  71.1 135.4 %reduce-scatter.45.cloned.1.call-start = ((), (), s32[]{:S(2)}) async-start(), calls=%async_computation.34 | async-start | bytes 589824 | tf_op jit(solution)/shard_map/reduce_scatter | solution.py:62
  71.6 4.8 copy-start.9
  84.7 3.5 copy-start.58
  89.9 2.8 copy-start.34
  95.5 10.5 %copy-start.26 = (bf16[1,128,512]{2,1,0:T(8,128)(2,1)S(1)}, bf16[1,128,512]{2,1,0:T(8,128)(2,1)}, u32[]{:S(2)}) copy-start(bf16[1,128,512]{2,1,0:T(8,128)(2,1)} %param.15) | copy-start | bytes 393220
  103.1 3.0 copy-start.43
  103.1 3.7 copy-start.27
  103.1 3.7 copy-start.56
  105.8 2.5 copy-start.46
  106.1 2.3 copy-start.55
  114.7 3.0 copy-start.35
  114.7 3.0 copy-start.39
  117.6 3.7 copy-start.5
  117.7 3.7 copy-start.6
  138.7 18.2 %all-to-all-start.2 = ((bf16[8,32,512]{2,1,0:T(8,128)(2,1)}), bf16[8,32,512]{2,1,0:T(8,128)(2,1)}, u32[]{:S(2)}, u32[]{:S(2)}) async-start(bf16[8,32,512]{2,1,0:T(8,128)(2,1)} %bitcast.29), calls=%async_computation.2 | async-start | bytes 524288 | tf_op jit(solution)/shard_map/all_to_all | solution.py:190
  144.6 93.4 %reduce-scatter.41.cloned.1.call-start = ((), (), s32[]{:S(2)}) async-start(), calls=%async_computation.32 | async-start | bytes 589824 | tf_op jit(solution)/shard_map/reduce_scatter | solution.py:62
  146.1 3.5 copy-start.37
  165.7 3.7 copy-start.29
  165.7 3.7 copy-start.31
  165.7 137.5 %reduce-scatter.29.cloned.1.call-start = ((), (), s32[]{:S(2)}) async-start(), calls=%async_computation.26 | async-start | bytes 589824 | tf_op jit(solution)/shard_map/reduce_scatter | solution.py:56
  169.3 198.8 %reduce-scatter.25.cloned.1.call-start = ((), (), s32[]{:S(2)}) async-start(), calls=%async_computation.24 | async-start | bytes 589824 | tf_op jit(solution)/shard_map/reduce_scatter | solution.py:56
  170.7 19.1 %copy-start.17 = (bf16[128,512]{1,0:T(8,128)(2,1)}, bf16[128,512]{1,0:T(8,128)(2,1)S(1)}, u32[]{:S(2)}) copy-start(bf16[128,512]{1,0:T(8,128)(2,1)S(1)} %fusion.7) | copy-start | bytes 393220
  177.0 2.9 copy-start.33
  177.0 2.9 copy-start.41
  180.0 4.7 copy-start.3
  187.9 246.6 %reduce-scatter.37.cloned.1.call-start = ((), (), s32[]{:S(2)}) async-start(), calls=%async_computation.30 | async-start | bytes 1179648 | tf_op jit(solution)/shard_map/reduce_scatter | solution.py:59
  189.7 311.2 %reduce-scatter.33.cloned.1.call-start = ((), (), s32[]{:S(2)}) async-start(), calls=%async_computation.28 | async-start | bytes 1179648 | tf_op jit(solution)/shard_map/reduce_scatter | solution.py:59
  190.1 2.6 copy-start.8
  192.6 378.1 %reduce-scatter.21.cloned.1.call-start = ((), (), s32[]{:S(2)}) async-start(), calls=%async_computation.22 | async-start | bytes 1769472 | tf_op jit(solution)/shard_map/reduce_scatter | solution.py:53
  192.7 2.1 copy-start.13
  198.0 3.5 copy-start.11
  198.0 440.5 %reduce-scatter.17.cloned.1.call-start = ((), (), s32[]{:S(2)}) async-start(), calls=%async_computation.20 | async-start | bytes 1769472 | tf_op jit(solution)/shard_map/reduce_scatter | solution.py:53
  201.5 233.1 %copy-start.14 = (bf16[1024,512]{1,0:T(8,128)(2,1)}, bf16[1024,512]{1,0:T(8,128)(2,1)S(1)}, u32[]{:S(2)}) copy-start(bf16[1024,512]{1,0:T(8,128)(2,1)S(1)} %multiply_convert_fusion) | copy-start | bytes 3145732
  205.1 98.1 %copy-start.61 = (u32[32]{0:T(128)S(1)}, u32[32]{0:T(128)}, u32[]{:S(2)}) copy-start(u32[32]{0:T(128)} %constant.49) | copy-start | bytes 388
  205.1 98.7 %copy-start.60 = (u32[32]{0:T(128)S(1)}, u32[32]{0:T(128)}, u32[]{:S(2)}) copy-start(u32[32]{0:T(128)} %constant.45) | copy-start | bytes 388
  205.1 100.6 %copy-start.48 = (bf16[512]{0:T(512)(128)(2,1)S(1)}, bf16[512]{0:T(512)(128)(2,1)}, u32[]{:S(2)}) copy-start(bf16[512]{0:T(512)(128)(2,1)} %get-tuple-element.16) | copy-start | bytes 3076
  205.1 100.6 %copy-start.49 = (bf16[512]{0:T(512)(128)(2,1)S(1)}, bf16[512]{0:T(512)(128)(2,1)}, u32[]{:S(2)}) copy-start(bf16[512]{0:T(512)(128)(2,1)} %get-tuple-element.8) | copy-start | bytes 3076
  205.2 100.6 %copy-start.50 = (bf16[512]{0:T(512)(128)(2,1)S(1)}, bf16[512]{0:T(512)(128)(2,1)}, u32[]{:S(2)}) copy-start(bf16[512]{0:T(512)(128)(2,1)} %get-tuple-element.14) | copy-start | bytes 3076
  205.2 100.6 %copy-start.51 = (bf16[512]{0:T(512)(128)(2,1)S(1)}, bf16[512]{0:T(512)(128)(2,1)}, u32[]{:S(2)}) copy-start(bf16[512]{0:T(512)(128)(2,1)} %get-tuple-element.10) | copy-start | bytes 3076
  206.5 452.8 %reduce-scatter.47.cloned.1.call-start = ((), (), s32[]{:S(2)}) async-start(), calls=%async_computation.35 | async-start | bytes 81920 | tf_op jit(solution)/shard_map/reduce_scatter | solution.py:82
  207.2 473.9 %reduce-scatter.43.cloned.1.call-start = ((), (), s32[]{:S(2)}) async-start(), calls=%async_computation.33 | async-start | bytes 81920 | tf_op jit(solution)/shard_map/reduce_scatter | solution.py:82
  238.0 465.1 %reduce-scatter.31.cloned.1.call-start = ((), (), s32[]{:S(2)}) async-start(), calls=%async_computation.27 | async-start | bytes 81920 | tf_op jit(solution)/shard_map/reduce_scatter | solution.py:76
  303.2 421.8 %reduce-scatter.27.cloned.1.call-start = ((), (), s32[]{:S(2)}) async-start(), calls=%async_computation.25 | async-start | bytes 81920 | tf_op jit(solution)/shard_map/reduce_scatter | solution.py:76
  368.2 378.9 %reduce-scatter.39.cloned.1.call-start = ((), (), s32[]{:S(2)}) async-start(), calls=%async_computation.31 | async-start | bytes 163840 | tf_op jit(solution)/shard_map/reduce_scatter | solution.py:79
  434.5 78.3 %copy-start.18 = (bf16[128,512]{1,0:T(8,128)(2,1)S(1)}, bf16[128,512]{1,0:T(8,128)(2,1)}, u32[]{:S(2)}) copy-start(bf16[128,512]{1,0:T(8,128)(2,1)} %copy-done.17) | copy-start | bytes 393220
  434.6 334.5 %reduce-scatter.35.cloned.1.call-start = ((), (), s32[]{:S(2)}) async-start(), calls=%async_computation.29 | async-start | bytes 163840 | tf_op jit(solution)/shard_map/reduce_scatter | solution.py:79
  509.2 136.6 %all-to-all-start.3 = ((bf16[8,32,512]{2,1,0:T(8,128)(2,1)}), bf16[8,32,512]{2,1,0:T(8,128)(2,1)S(1)}, u32[]{:S(2)}, u32[]{:S(2)}) async-start(bf16[8,32,512]{2,1,0:T(8,128)(2,1)} %bitcast.31), calls=%async_computation.3 | async-start | bytes 524288 | tf_op jit(solution)/shard_map/all_to_all | solution.py:190
  512.8 278.3 %reduce-scatter.23.cloned.1.call-start = ((), (), s32[]{:S(2)}) async-start(), calls=%async_computation.23 | async-start | bytes 245760 | tf_op jit(solution)/shard_map/reduce_scatter | solution.py:73
  570.7 242.6 %reduce-scatter.19.cloned.1.call-start = ((), (), s32[]{:S(2)}) async-start(), calls=%async_computation.21 | async-start | bytes 245760 | tf_op jit(solution)/shard_map/reduce_scatter | solution.py:73
  648.2 166.6 %copy-start = (f32[128,512]{1,0:T(8,128)}, f32[128,512]{1,0:T(8,128)S(1)}, u32[]{:S(2)}) copy-start(f32[128,512]{1,0:T(8,128)S(1)} %scatter_custom_fusion.7) | copy-start | bytes 786436
  (18 other events, 24.6 us)
Sparse Core Ops, SparseCore 0:
  108.5 64.4 reduce-scatter.44
  176.3 61.5 reduce-scatter.40
  241.3 61.7 reduce-scatter.28
  306.4 61.7 reduce-scatter.24
  371.4 63.0 reduce-scatter.36
  437.8 63.1 reduce-scatter.32
  504.4 66.2 reduce-scatter.20
  574.1 64.3 reduce-scatter.16
  640.9 18.3 reduce-scatter.46
  661.5 19.5 reduce-scatter.42
  683.5 19.5 reduce-scatter.30
  705.4 19.5 reduce-scatter.26
  727.4 19.6 reduce-scatter.38
  749.4 19.6 reduce-scatter.34
  771.3 19.7 reduce-scatter.22
  793.4 19.7 reduce-scatter.18
where the time goes:
time: 831 us; the launch traced here: 822 us
  waiting for transfers between devices  545 us (66%)
  other arithmetic  74.6 us (9%)
  matrix products  72.7 us (9%)
  local copies, waits for them, and re-layouts  62.7 us (8%)
  blocking collectives  25.3 us (3%)
  starting transfers between devices  23.8 us (3%)
  between operations  17.3 us (2%)
    reduce_scatter x2, waiting for transfers between devices, reduce_terms(): lax.psum_scatter(terms[2].astype(jnp.bfloat16), 'graph', scatter_dimensio...  129 us
    reduce_scatter x2, waiting for transfers between devices, reduce_terms(): lax.psum_scatter(terms[0].astype(jnp.bfloat16), 'graph', scatter_dimensio...  122 us
    reduce_scatter x2, waiting for transfers between devices, reduce_terms(): lax.psum_scatter(terms[1].astype(jnp.bfloat16), 'graph', scatter_dimensio...  102 us
    reduce_scatter x2, waiting for transfers between devices, reduce_terms(): lax.psum_scatter(partial_sum[0].astype(jnp.bfloat16), 'batch', scatter_di...  42.8 us
    reduce_scatter x2, waiting for transfers between devices, reduce_terms(): lax.psum_scatter(partial_sum[2].astype(jnp.bfloat16), 'batch', scatter_di...  42.7 us
    reduce_scatter x2, waiting for transfers between devices, reduce_terms(): lax.psum_scatter(partial_sum[1].astype(jnp.bfloat16), 'batch', scatter_di...  42.5 us
    reduce_scatter x2, waiting for transfers between devices, reduce_terms(): lax.psum_scatter(partial_sum[3].astype(jnp.bfloat16), 'batch', scatter_di...  32.9 us
    reduce_scatter x2, waiting for transfers between devices, reduce_terms(): lax.psum_scatter(terms[3].astype(jnp.bfloat16), 'graph', scatter_dimensio...  30.7 us
  transfers between devices with their start and end apart: 20, of which 16 were waited for; matrix products, arithmetic and copies ran while one was open for 17% of the time, Pallas kernels for 0%

commit v1 on v0

v1 whole, which is shorter than its diff:
```python
import functools

import jax
import jax.numpy as jnp
from jax import lax
from jax.experimental import pallas as pl
from jax.experimental.pallas import tpu as pltpu
from jax.sharding import PartitionSpec as P

EPSILON = 1e-05
BF = jnp.bfloat16
F32 = jnp.float32


def dot(a, b):
    return jnp.dot(a, b, preferred_element_type=F32)


def dot_t(a, b):
    return lax.dot_general(a, b, (((0,), (0,)), ((), ())), preferred_element_type=F32)


def dot_nt(a, b):
    return lax.dot_general(a, b, (((1,), (1,)), ((), ())), preferred_element_type=F32)


def head(pre_act, w_out, gain):
    hidden = (pre_act * jax.nn.sigmoid(pre_act)).astype(BF)
    projected = dot(hidden, w_out)
    centre = projected - jnp.mean(projected, axis=-1, keepdims=True)
    inv_std = lax.rsqrt(jnp.mean(centre * centre, axis=-1, keepdims=True) + EPSILON)
    normed = centre * inv_std
    return normed * gain, (pre_act, hidden, normed, inv_std)


def head_backward(grad_out, w_out, gain, saved):
    pre_act, hidden, normed, inv_std = saved
    grad_gain = jnp.sum(grad_out * normed, axis=0)
    grad_norm = grad_out * gain
    grad_proj = inv_std * (
        grad_norm
        - jnp.mean(grad_norm, axis=-1, keepdims=True)
        - normed * jnp.mean(grad_norm * normed, axis=-1, keepdims=True)
    )
    grad_proj_bf = grad_proj.astype(BF)
    grad_w_out = dot_t(hidden, grad_proj_bf)
    grad_hidden = dot_nt(grad_proj_bf, w_out)
    sigma = jax.nn.sigmoid(pre_act)
    grad_pre = (grad_hidden * sigma * (1.0 + pre_act * (1.0 - sigma))).astype(BF)
    return grad_pre, grad_w_out, grad_gain


def exchange(rows):
    return lax.all_to_all(rows, "graph", split_axis=0, concat_axis=0, tiled=True)


def lane_orders(groups, samples):
    batch_bits = [("batch", k) for k in range(samples.bit_length() - 1)]
    graph_bits = [("graph", k) for k in range(groups.bit_length() - 1)]
    first = batch_bits + graph_bits
    second = batch_bits[:1] + graph_bits[:1] + batch_bits[1:] + graph_bits[:0:-1]
    return first, second


def pack(terms, order, groups, samples):
    parts = groups * samples
    width = terms[0].shape[1]
    blocks = [t.astype(BF).reshape(parts, -1, width) for t in terms[:4]]
    gains = jnp.stack([t.astype(BF).reshape(parts, -1) for t in terms[4:]], axis=1)
    gains = jnp.pad(gains, ((0, 0), (0, 8 - gains.shape[1]), (0, width - gains.shape[2])))
    packed = jnp.concatenate(blocks + [gains], axis=1)
    bits = len(order)
    natural = [("graph", k) for k in range(groups.bit_length() - 1)][::-1]
    natural += [("batch", k) for k in range(samples.bit_length() - 1)][::-1]
    axes = [natural.index(bit) for bit in order]
    split = packed.reshape((2,) * bits + packed.shape[1:])
    return split.transpose(axes + [bits, bits + 1]).reshape(packed.shape)


def halving_kernel(orders, *refs):
    lanes = len(orders)
    steps = len(orders[0])
    sources, out_ref = refs[:lanes], refs[lanes]
    rest = refs[lanes + 1 :]
    landed = [rest[lane * steps : (lane + 1) * steps] for lane in range(lanes)]
    send_sem, recv_sem = rest[lanes * steps :]
    position = {"batch": lax.axis_index("batch"), "graph": lax.axis_index("graph")}

    def bit_of(axis, bit):
        return lax.rem(lax.div(position[axis], 2**bit), 2)

    def partner(axis, bit):
        return {axis: position[axis] + 2**bit * (1 - 2 * bit_of(axis, bit))}

    barrier = pltpu.get_barrier_semaphore()
    for axis, bit in orders[0]:
        pl.semaphore_signal(
            barrier, inc=1, device_id=partner(axis, bit), device_id_type=pl.DeviceIdType.MESH
        )
    pl.semaphore_wait(barrier, steps)

    def send(lane, step):
        axis, bit = orders[lane][step]
        source = sources[lane] if step == 0 else landed[lane][step - 1]
        half = source.shape[0] // 2
        copy = pltpu.make_async_remote_copy(
            src_ref=source.at[pl.ds((1 - bit_of(axis, bit)) * half, half)],
            dst_ref=landed[lane][step],
            send_sem=send_sem.at[lane * steps + step],
            recv_sem=recv_sem.at[lane * steps + step],
            device_id=partner(axis, bit),
            device_id_type=pl.DeviceIdType.MESH,
        )
        copy.start()
        return copy

    def accumulate(lane, step, start, count):
        source = sources[lane] if step == 0 else landed[lane][step - 1]
        target = landed[lane][step]
        base = bit_of(*orders[lane][step]) * target.shape[0]

        def add(i, carry):
            mine = source[base + start + i].astype(F32)
            target[start + i] = (mine + target[start + i].astype(F32)).astype(BF)
            return carry

        lax.fori_loop(0, count, add, 0)

    flying = [send(lane, 0) for lane in range(lanes)]
    started = list(flying)
    for step in range(steps):
        for lane in range(lanes):
            flying[lane].wait_recv()
            count = landed[lane][step].shape[0]
            if step + 1 < steps:
                half = count // 2
                keep = bit_of(*orders[lane][step + 1])
                accumulate(lane, step, (1 - keep) * half, half)
                flying[lane] = send(lane, step + 1)
                started.append(flying[lane])
                accumulate(lane, step, keep * half, half)
            else:
                base = bit_of(*orders[lane][step])
                last = landed[lane][step - 1]
                out_ref[lane] = last[base].astype(F32) + landed[lane][step][0].astype(F32)
    for copy in started:
        copy.wait_send()


def reduce_terms(layer_terms):
    groups = lax.axis_size("graph")
    samples = lax.axis_size("batch")
    parts = groups * samples
    choices = lane_orders(groups, samples)
    orders = [choices[i % 2] for i in range(len(layer_terms))]
    packed = [pack(t, o, groups, samples) for t, o in zip(layer_terms, orders)]
    count, per, width = packed[0].shape
    steps = len(orders[0])
    copies = len(orders) * steps
    total = pl.pallas_call(
        functools.partial(halving_kernel, orders),
        out_shape=jax.ShapeDtypeStruct((len(orders), per, width), F32),
        in_specs=[pl.BlockSpec(memory_space=pltpu.VMEM)] * len(orders),
        out_specs=pl.BlockSpec(memory_space=pltpu.VMEM),
        scratch_shapes=[
            pltpu.VMEM((count >> (step + 1), per, width), BF)
            for _ in orders
            for step in range(steps)
        ]
        + [pltpu.SemaphoreType.DMA((copies,)), pltpu.SemaphoreType.DMA((copies,))],
        compiler_params=pltpu.CompilerParams(
            collective_id=0, has_side_effects=True, vmem_limit_bytes=48 * 1024 * 1024
        ),
    )(*packed)
    out = []
    at = 0
    for t in layer_terms[0][:4]:
        rows = t.shape[0] // parts
        out.append(total[:, at : at + rows])
        at += rows
    share = layer_terms[0][4].shape[0] // parts
    out.append(total[:, at, :share])
    out.append(total[:, at + 1, :share])
    return tuple(out)


def body(
    node_latent,
    edge_latent,
    node_cotangent,
    edge_w_in,
    edge_w_out,
    node_w_in,
    node_w_out,
    edge_gain,
    node_gain,
    edge_slot,
    edge_receiver,
    send_list,
    edge_count,
):
    width = node_latent.shape[2]
    node_rows = node_latent.shape[1]
    slots = edge_slot.shape[0]
    groups = lax.axis_size("graph")
    peer_rows = send_list.shape[1]
    remote_rows = groups * peer_rows
    layers = edge_w_in.shape[0]
    live = (jnp.arange(slots, dtype=jnp.int32) < edge_count[0])[:, None]
    at_recv = (
        edge_receiver[:, None] == jnp.arange(node_rows, dtype=jnp.int32)[None, :]
    ).astype(BF)
    at_send = (
        edge_slot[:, None] == jnp.arange(node_rows + remote_rows, dtype=jnp.int32)[None, :]
    ).astype(BF)
    pick = jnp.concatenate([at_recv, at_send], axis=1)
    listed = (
        send_list.reshape(-1)[:, None] == jnp.arange(node_rows, dtype=jnp.int32)[None, :]
    ).astype(BF)
    live_f = live.astype(F32)
    state = node_latent[0].astype(F32)
    edge_state = edge_latent[0].astype(F32)
    edge_bf = edge_latent[0]
    records = []
    for layer in range(layers):
        node_bf = state.astype(BF)
        if layer > 0:
            edge_bf = edge_state.astype(BF)
        w_first = edge_w_in[layer]
        from_send = dot(node_bf, w_first[width : 2 * width]).astype(BF)
        from_recv = dot(node_bf, w_first[2 * width :]).astype(BF)
        arrived = exchange(dot(listed, from_send).astype(BF))
        table = jnp.concatenate([from_recv, from_send, arrived], axis=0)
        pre = dot(edge_bf, w_first[:width]) + dot(pick, table)
        message, edge_saved = head(pre, edge_w_out[layer], edge_gain[layer])
        message = message * live_f
        summed = dot_t(at_recv, message.astype(BF)).astype(BF)
        n_first = node_w_in[layer]
        n_pre = dot(node_bf, n_first[:width]) + dot(summed, n_first[width:])
        update, node_saved = head(n_pre, node_w_out[layer], node_gain[layer])
        records.append((edge_bf, node_bf, summed, edge_saved, node_saved))
        if layer + 1 < layers:
            edge_state = edge_state + message
        state = state + update
    grad_state = node_cotangent[0].astype(F32)
    grad_edge = None
    reduced = []
    for layer in reversed(range(layers)):
        edge_bf, node_bf, summed, edge_saved, node_saved = records[layer]
        w_first = edge_w_in[layer]
        n_first = node_w_in[layer]
        n_pre_g, grad_n_out, grad_n_gain = head_backward(
            grad_state, node_w_out[layer], node_gain[layer], node_saved
        )
        grad_state = grad_state + dot_nt(n_pre_g, n_first[:width])
        grad_sum = dot_nt(n_pre_g, n_first[width:]).astype(BF)
        grad_n_in = jnp.concatenate([dot_t(node_bf, n_pre_g), dot_t(summed, n_pre_g)], axis=0)
        grad_message = dot(at_recv, grad_sum)
        if grad_edge is not None:
            grad_message = grad_message + grad_edge
        e_pre_g, grad_e_out, grad_e_gain = head_backward(
            grad_message * live_f, edge_w_out[layer], edge_gain[layer], edge_saved
        )
        gathered = dot_t(pick, e_pre_g)
        outgoing = gathered[2 * node_rows :].astype(BF)
        arrived = exchange(outgoing)
        if layer > 0:
            part = dot_nt(e_pre_g, w_first[:width])
            grad_edge = part if grad_edge is None else part + grad_edge
        sum_recv = gathered[:node_rows].astype(BF)
        sum_send = (gathered[node_rows : 2 * node_rows] + dot_t(listed, arrived)).astype(BF)
        grad_state = (
            grad_state
            + dot_nt(sum_send, w_first[width : 2 * width])
            + dot_nt(sum_recv, w_first[2 * width :])
        )
        grad_e_in = jnp.concatenate(
            [dot_t(edge_bf, e_pre_g), dot_t(node_bf, sum_send), dot_t(node_bf, sum_recv)], axis=0
        )
        reduced.append(
            (grad_e_in, grad_e_out, grad_n_in, grad_n_out, grad_e_gain, grad_n_gain)
        )
    return (state[None], grad_state[None]) + reduce_terms(reduced[::-1])


def solution(mesh):
    node = P("batch", "graph", None)
    in_specs = (node, node, node) + (P(),) * 6 + (P("graph"), P("graph"), P("graph", None), P("graph"))
    weight = P(None, ("graph", "batch"), None)
    gain = P(None, ("graph", "batch"))
    out_specs = (node, node, weight, weight, weight, weight, gain, gain)
    return jax.shard_map(body, mesh=mesh, in_specs=in_specs, out_specs=out_specs, check_vma=False)
```

time: 831 us -> 208 us (0.25)
  waiting for transfers between devices: 545 us -> 5.78 us
  Pallas kernels: 0 us -> 65.8 us
  other arithmetic: 74.6 us -> 13.6 us
  local copies, waits for them, and re-layouts: 62.7 us -> 24.1 us
  blocking collectives: 25.3 us -> 0 us
  between operations: 17.3 us -> 2.3 us
    reduce_scatter x16 -> x0, waiting for transfers between devices: 544 us -> none  [the longest x2 129 us: reduce_terms(): lax.psum_scatter(terms[2].astype(jnp.bfloat16), 'graph', scatter_dimensio...]
    pallas_call x0 -> x1, Pallas kernels: none -> 65.8 us  [reduce_terms(): pl.pallas_call(functools.partial(halving_kernel, orders), out_shape=jax.S...]
    scatter-add x8 -> x0, other arithmetic: 49.8 us -> none  [the longest x2 15.6 us: body(): jax.ops.segment_sum(edge_parts[2], edge_slot, num_segments=buffer_rows)]
    gather x10 -> x0, local copies, waits for them, and re-layouts: 40.7 us -> none  [the longest x4 15.7 us: body(): grad_message = node_parts[1][edge_receiver]]
    unnamed x2 -> x0, blocking collectives: 25.3 us -> none
    dot_general x41 -> x51, matrix products: 72.7 us -> 74.4 us  [the longest x20 31.8 us: dot(): return jnp.dot(a, b, preferred_element_type=F32)]
  transfers between devices with their start and end apart: 20 -> 4, of which waited for: 16 -> 2; matrix products, arithmetic and copies ran while one was open for 17% -> 13% of each run, Pallas kernels for 0% -> 0%
where the time goes in v1:
time: 208 us; the launch traced here: 207 us
  matrix products  74.4 us (36%)
  Pallas kernels  65.8 us (32%)
  local copies, waits for them, and re-layouts  24.1 us (12%)
  starting transfers between devices  21 us (10%)
  other arithmetic  13.6 us (7%)
  waiting for transfers between devices  5.78 us (3%)
  between operations  2.3 us (1%)
    pallas_call x1, Pallas kernels, reduce_terms(): pl.pallas_call(functools.partial(halving_kernel, orders), out_shape=jax.S...  65.8 us
    dot_general x20, matrix products, dot(): return jnp.dot(a, b, preferred_element_type=F32)  31.8 us
    dot_general x20, matrix products, dot_t(): lax.dot_general(a, b, (((0,), (0,)), ((), ())), preferred_element_type=F32)  26 us
    all_to_all x4, starting transfers between devices, exchange(): lax.all_to_all(rows, 'graph', split_axis=0, concat_axis=0, tiled=True)  21 us
    dot_general x11, matrix products, dot_nt(): lax.dot_general(a, b, (((1,), (1,)), ((), ())), preferred_element_type=F32)  16.6 us
    unnamed x181, local copies, waits for them, and re-layouts  12.5 us
    all_to_all x4, waiting for transfers between devices, exchange(): lax.all_to_all(rows, 'graph', split_axis=0, concat_axis=0, tiled=True)  5.78 us
    convert_element_type x3, other arithmetic, head_backward(): grad_proj_bf = grad_proj.astype(BF)  4.53 us
  transfers between devices with their start and end apart: 4, of which 2 were waited for; matrix products, arithmetic and copies ran while one was open for 13% of the time, Pallas kernels for 0%

profile of v1, /device:TPU:0, one launch (start us, length us, event | category | flops | bytes accessed | tf_op | source)
XLA Modules:
  0.0 206.8 jit_solution(12145074412315112423)
XLA Ops:
  0.7 0.9 eq.47
  1.6 1.3 convolution_convert_fusion.20
  2.9 1.0 convolution_convert_fusion.15
  3.9 7.3 %all-to-all-start = ((bf16[8,32,512]{2,1,0:T(8,128)(2,1)}), bf16[8,32,512]{2,1,0:T(8,128)(2,1)}, u32[]{:S(2)}, u32[]{:S(2)}) async-start(bf16[8,32,512]{2,1,0:T(8,128)(2,1)} %bitcast.6), calls=%async_computation | async-start | bytes 524288 | tf_op jit(solution)/shard_map/all_to_all | solution.py:54
  11.2 2.0 convolution_convert_fusion.21
  14.0 2.0 fusion.67
  16.0 1.0 iota_compare_fusion
  18.3 1.3 copy.30
  19.6 1.7 fusion.17
  21.4 1.9 convolution_add_fusion.1
  23.3 0.9 fusion.139
  27.4 1.3 convolution_convert_fusion.18
  28.8 0.9 fusion.50
  30.4 1.0 convolution_convert_fusion.14
  31.4 6.0 %all-to-all-start.1 = ((bf16[8,32,512]{2,1,0:T(8,128)(2,1)}), bf16[8,32,512]{2,1,0:T(8,128)(2,1)}, u32[]{:S(2)}, u32[]{:S(2)}) async-start(bf16[8,32,512]{2,1,0:T(8,128)(2,1)} %bitcast.208), calls=%async_computation.1 | async-start | bytes 524288 | tf_op jit(solution)/shard_map/all_to_all | solution.py:54
  37.4 2.0 convolution_convert_fusion.19
  39.4 3.1 %fusion.47 = f32[1024,512]{1,0:T(8,128)} fusion(bf16[1024,512]{0,1:T(8,128)(2,1)S(1)} %add_convert_fusion, bf16[2,1536,512]{2,1,0:T(8,128)(2,1)} %param.16), kind=kOutput, calls=%fused_computation.111 | convolution fusion | flops 536870912 | bytes 3670016 | tf_op jit(solution)/shard_map/dot_general | solution.py:16
  42.5 3.5 %all-to-all-done.1 = bf16[8,32,512]{2,1,0:T(8,128)(2,1)} async-done(((bf16[8,32,512]{2,1,0:T(8,128)(2,1)}), bf16[8,32,512]{2,1,0:T(8,128)(2,1)}, u32[]{:S(2)}, u32[]{:S(2)}) %all-to-all-start.1) | async-done | bytes 262176 | tf_op jit(solution)/shard_map/all_to_all | solution.py:54
  46.0 2.7 %convolution_add_fusion = f32[1024,512]{1,0:T(8,128)S(1)} fusion(f32[1024,512]{1,0:T(8,128)} %fusion.47, bf16[256,512]{1,0:T(8,128)(2,1)} %bitcast.19, bf16[128,512]{1,0:T(8,128)(2,1)} %copy-done.37, bf16[128,512]{1,0:T(8,128)(2,1)} %convolution_convert_fusion.19, pred[1024,384]{1,0:T(32,128)(4,1)} %iota_compare_fusion, pred[1024,128]{1,0:T(32,128)(4,1)} %copy-done.24), kind=kOutput, calls=%fused_computation.24 | convolution fusion | flops 539492352 | bytes 5242880 | tf_op jit(solution)/shard_map/dot_general | solution.py:16
  48.8 0.8 fusion.141
  51.1 0.8 convolution_convert_fusion.22
  54.5 1.2 convolution_convert_fusion.1
  55.7 1.0 convolution_add_fusion.9
  56.8 1.1 convolution_convert_fusion.2
  57.9 1.1 convolution_convert_fusion.3
  59.0 4.8 %multiply_reduce_fusion = (bf16[512]{0:T(512)(128)(2,1)}, f32[1024]{0:T(1024)}, f32[1024]{0:T(1024)}, f32[1024,512]{0,1:T(8,128)}) fusion(f32[1024,512]{0,1:T(8,128)} %copy-done, f32[1024]{0:T(1024)} %copy-done.62, f32[1024]{0:T(1024)S(1)} %broadcast_multiply_fusion.4, f32[1024]{0:T(1024)S(1)} %fusion.128, f32[512]{0:T(512)} %bitcast.224, ...), kind=kOutput, calls=%fused_computation | convolution fusion | flops 206239232 | bytes 4877312 | tf_op jit(solution)/shard_map/dot_general | solution.py:16
  65.2 3.0 %multiply_convert_fusion.3 = bf16[1024,512]{0,1:T(8,128)(2,1)S(1)} fusion(f32[1024,512]{0,1:T(8,128)} %get-tuple-element.38, f32[1024,512]{0,1:T(8,128)} %copy-done, f32[1024]{0:T(1024)S(1)} %broadcast_multiply_fusion.2, f32[1024]{0:T(1024)S(1)} %broadcast_multiply_fusion.3, f32[512]{0:T(512)} %bitcast.225, f32[1024]{0:T(1024)} %copy-done.62, ...), kind=kLoop, calls=%fused_computation.7 | loop fusion | flops 4718592 | bytes 5265408 | tf_op jit(solution)/shard_map/convert_element_type | solution.py:45
  68.3 1.3 multiply_convert_fusion.2
  69.6 1.6 convolution_convert_fusion.7
  71.2 1.8 fusion.145
  73.8 1.1 convolution_convert_fusion.5
  75.8 4.3 %all-to-all-start.2 = ((bf16[8,32,512]{2,1,0:T(8,128)(2,1)}), bf16[8,32,512]{2,1,0:T(8,128)(2,1)}, u32[]{:S(2)}, u32[]{:S(2)}) async-start(bf16[8,32,512]{2,1,0:T(8,128)(2,1)} %bitcast.28), calls=%async_computation.2 | async-start | bytes 524288 | tf_op jit(solution)/shard_map/all_to_all | solution.py:54
  80.1 1.4 pad_maximum_fusion.3
  81.5 1.4 pad.8.clone
  82.9 2.9 %convolution_convert_fusion.4 = bf16[512,512]{1,0:T(8,128)(2,1)} fusion(bf16[1024,512]{0,1:T(8,128)(2,1)} %copy-done.35, f32[1024,512]{1,0:T(8,128)S(1)} %copy-done.20), kind=kOutput, calls=%fused_computation.34 | convolution fusion | flops 539754496 | bytes 3670016 | tf_op jit(solution)/shard_map/dot_general | solution.py:20
  85.8 2.3 %all-to-all-done.2 = bf16[8,32,512]{2,1,0:T(8,128)(2,1)} async-done(((bf16[8,32,512]{2,1,0:T(8,128)(2,1)}), bf16[8,32,512]{2,1,0:T(8,128)(2,1)}, u32[]{:S(2)}, u32[]{:S(2)}) %all-to-all-start.2) | async-done | bytes 262176 | tf_op jit(solution)/shard_map/all_to_all | solution.py:54
  88.1 1.4 fusion.9
  89.5 1.5 convolution_add_fusion.7
  91.0 2.1 multiply_reduce_fusion.7
  93.1 0.9 multiply_convert_fusion.8
  94.4 1.1 convolution_convert_fusion.8
  95.5 1.1 convolution_convert_fusion.6
  96.7 2.0 convolution_add_fusion.5
  98.7 1.1 convolution_convert_fusion.9
  99.9 1.2 fusion.5
  101.0 3.1 %fusion.14 = f32[1024,512]{0,1:T(8,128)} fusion(bf16[128,512]{1,0:T(8,128)(2,1)S(1)} %fusion.11, bf16[2,1024,512]{2,1,0:T(8,128)(2,1)} %param.18, s32[1024]{0:T(1024)S(1)} %copy-done.61), kind=kOutput, calls=%fused_computation.78 | convolution fusion | flops 201523200 | bytes 2756608 | tf_op jit(solution)/shard_map/dot_general | solution.py:16
  104.2 3.3 %multiply_reduce_fusion.1 = (bf16[512]{0:T(512)(128)(2,1)S(1)}, f32[1024]{0:T(1024)S(1)}, f32[1024]{0:T(1024)S(1)}, f32[1024,512]{0,1:T(8,128)S(1)}) fusion(f32[1024,512]{0,1:T(8,128)S(1)} %get-tuple-element.31, f32[1024]{0:T(1024)S(1)} %add_rsqrt_fusion.1, f32[1024]{0:T(1024)S(1)} %broadcast_multiply_fusion.5, f32[512]{0:T(512)S(1)} %bitcast.215, ...), kind=kOutput, calls=%fused_computation.1 | convolution fusion | flops 542111232 | bytes 7887872 | tf_op jit(solution)/shard_map/dot_general | solution.py:24
  108.1 1.0 copy-done.16
  109.3 1.3 multiply_convert_fusion
  111.0 1.5 fusion.2
  112.5 1.7 fusion.146
  115.0 1.1 fusion.4
  117.1 3.4 %all-to-all-start.3 = ((bf16[8,32,512]{2,1,0:T(8,128)(2,1)}), bf16[8,32,512]{2,1,0:T(8,128)(2,1)S(1)}, u32[]{:S(2)}, u32[]{:S(2)}) async-start(bf16[8,32,512]{2,1,0:T(8,128)(2,1)} %bitcast.30), calls=%async_computation.3 | async-start | bytes 524288 | tf_op jit(solution)/shard_map/all_to_all | solution.py:54
  120.5 1.3 pad_maximum_fusion.1
  122.0 0.9 copy-done.40
  123.9 2.4 %copy.44 = bf16[2,2,2,2,2,120,512]{6,5,1,0,3,2,4:T(8,128)(2,1)} copy(bf16[2,2,2,2,2,120,512]{6,5,4,3,2,1,0:T(8,128)(2,1)S(1)} %constant_dynamic-update-slice_fusion.5) | data formatting | bytes 7864320 | tf_op jit(solution)/shard_map/concatenate | solution.py:71
  126.3 1.5 copy-done.17
  127.9 1.6 convolution_convert_fusion.11
  129.5 1.2 fusion.10
  131.1 1.3 pad_maximum_fusion
  132.6 0.9 copy-done.43
  135.0 65.8 %shard_map.188 = f32[2,120,512]{2,1,0:T(8,128)S(1)} custom-call(bf16[32,120,512]{2,1,0:T(8,128)(2,1)S(1)} %bitcast.199, bf16[32,120,512]{2,1,0:T(8,128)(2,1)} %bitcast.200), custom_call_target="tpu_custom_call" | custom-call | tf_op jit(solution)/shard_map/pallas_call | solution.py:160
  203.3 1.3 convolution_add_fusion.3
  204.7 2.1 %fusion.6 = f32[1,128,512]{2,1,0:T(8,128)} fusion(f32[128,512]{1,0:T(8,128)S(1)} %convolution_add_fusion.3, bf16[2,1536,512]{2,1,0:T(8,128)(2,1)} %param.16, bf16[512,512]{1,0:T(8,128)(2,1)} %copy-done.41), kind=kOutput, calls=%fused_computation.51 | convolution fusion | flops 67174400 | bytes 1179648 | tf_op jit(solution)/shard_map/dot_general | solution.py:24
  (230 shorter events, 21.3 us)
Async XLA Ops:
  0.6 13.3 %copy-start.3 = (bf16[1,128,512]{2,1,0:T(8,128)(2,1)S(1)}, bf16[1,128,512]{2,1,0:T(8,128)(2,1)}, u32[]{:S(2)}) copy-start(bf16[1,128,512]{2,1,0:T(8,128)(2,1)} %param.13) | copy-start | bytes 393220
  0.6 12.5 %copy-start.73 = (f32[2,512]{1,0:T(2,128)S(1)}, f32[2,512]{1,0:T(2,128)}, u32[]{:S(2)}) copy-start(f32[2,512]{1,0:T(2,128)} %param.20) | copy-start | bytes 12292
  0.7 13.1 %copy-start.58 = (s32[1024]{0:T(1024)S(1)}, s32[1024]{0:T(1024)}, u32[]{:S(2)}) copy-start(s32[1024]{0:T(1024)} %param.23) | copy-start | bytes 12292
  0.7 15.3 %copy-start.70 = (s32[1024]{0:T(1024)S(1)}, s32[1024]{0:T(1024)}, u32[]{:S(2)}) copy-start(s32[1024]{0:T(1024)} %param.22) | copy-start | bytes 12292
  0.7 16.3 %copy-start.74 = (f32[2,512]{1,0:T(2,128)S(1)}, f32[2,512]{1,0:T(2,128)}, u32[]{:S(2)}) copy-start(f32[2,512]{1,0:T(2,128)} %param.21) | copy-start | bytes 12292
  0.7 17.6 %copy-start.4 = (bf16[1,1024,512]{2,1,0:T(8,128)(2,1)S(1)}, bf16[1,1024,512]{2,1,0:T(8,128)(2,1)}, u32[]{:S(2)}) copy-start(bf16[1,1024,512]{2,1,0:T(8,128)(2,1)} %param.14) | copy-start | bytes 3145732
  1.6 11.6 %copy-start.53 = (s32[256]{0:T(256)}, s32[256]{0:T(256)S(1)}, u32[]{:S(2)}) copy-start(s32[256]{0:T(256)S(1)} %eq.47) | copy-start | bytes 3076
  3.9 17.5 %all-to-all-start = ((bf16[8,32,512]{2,1,0:T(8,128)(2,1)}), bf16[8,32,512]{2,1,0:T(8,128)(2,1)}, u32[]{:S(2)}, u32[]{:S(2)}) async-start(bf16[8,32,512]{2,1,0:T(8,128)(2,1)} %bitcast.6), calls=%async_computation | async-start | bytes 524288 | tf_op jit(solution)/shard_map/all_to_all | solution.py:54
  13.7 16.0 %copy-start.49 = (f32[1,512]{1,0:T(1,128)}, f32[1,512]{1,0:T(1,128)S(1)}, u32[]{:S(2)}) copy-start(f32[1,512]{1,0:T(1,128)S(1)} %get-tuple-element.29) | copy-start | bytes 6148
  13.9 7.4 %copy-start.24 = (pred[1024,128]{1,0:T(32,128)(4,1)}, pred[1024,128]{1,0:T(32,128)(4,1)S(1)}, u32[]{:S(2)}) copy-start(pred[1024,128]{1,0:T(32,128)(4,1)S(1)} %iota_compare_fusion.1) | copy-start | bytes 393220
  21.4 1.9 copy-start.81
  24.7 1.6 copy-start.1
  24.7 1.6 copy-start.34
  25.0 1.7 copy-start.78
  26.3 2.4 %copy-start.44 = (bf16[128,512]{1,0:T(8,128)(2,1)}, bf16[128,512]{1,0:T(8,128)(2,1)S(1)}, u32[]{:S(2)}) copy-start(bf16[128,512]{1,0:T(8,128)(2,1)S(1)} %convolution_convert_fusion.23) | copy-start | bytes 393220
  26.7 2.0 copy-start.47
  26.7 3.0 %copy-start.6 = (bf16[1,1024,512]{1,2,0:T(8,128)(2,1)S(1)}, bf16[1,1024,512]{1,2,0:T(8,128)(2,1)}, u32[]{:S(2)}) copy-start(bf16[1,1024,512]{1,2,0:T(8,128)(2,1)} %copy.30) | copy-start | bytes 3145732
  27.0 1.7 copy-start.63
  31.4 14.6 %all-to-all-start.1 = ((bf16[8,32,512]{2,1,0:T(8,128)(2,1)}), bf16[8,32,512]{2,1,0:T(8,128)(2,1)}, u32[]{:S(2)}, u32[]{:S(2)}) async-start(bf16[8,32,512]{2,1,0:T(8,128)(2,1)} %bitcast.208), calls=%async_computation.1 | async-start | bytes 524288 | tf_op jit(solution)/shard_map/all_to_all | solution.py:54
  46.0 2.7 %copy-start.82 = (bf16[2,512,512]{2,1,0:T(8,128)(2,1)S(1)}, bf16[2,512,512]{2,1,0:T(8,128)(2,1)}, u32[]{:S(2)}) copy-start(bf16[2,512,512]{2,1,0:T(8,128)(2,1)} %param.17) | copy-start | bytes 3145732
  50.1 1.8 copy-start
  50.1 2.4 %copy-start.2 = (bf16[2,1024,512]{2,1,0:T(8,128)(2,1)S(1)}, bf16[2,1024,512]{2,1,0:T(8,128)(2,1)}, u32[]{:S(2)}) copy-start(bf16[2,1024,512]{2,1,0:T(8,128)(2,1)} %param.18) | copy-start | bytes 6291460
  50.1 2.4 %copy-start.33 = (f32[128,512]{1,0:T(8,128)S(1)}, f32[128,512]{1,0:T(8,128)}, u32[]{:S(2)}) copy-start(f32[128,512]{1,0:T(8,128)} %fusion.50) | copy-start | bytes 786436
  50.4 2.4 %copy-start.79 = (bf16[2,512,512]{2,1,0:T(8,128)(2,1)S(1)}, bf16[2,512,512]{2,1,0:T(8,128)(2,1)}, u32[]{:S(2)}) copy-start(bf16[2,512,512]{2,1,0:T(8,128)(2,1)} %param.19) | copy-start | bytes 3145732
  53.1 2.6 %copy-start.13 = (f32[128,512]{1,0:T(8,128)}, f32[128,512]{1,0:T(8,128)S(1)}, u32[]{:S(2)}) copy-start(f32[128,512]{1,0:T(8,128)S(1)} %get-tuple-element.37) | copy-start | bytes 786436
  53.2 2.6 %copy-start.68 = (f32[128]{0:T(128)}, f32[128]{0:T(128)S(1)}, u32[]{:S(2)}) copy-start(f32[128]{0:T(128)S(1)} %broadcast_multiply_fusion.10) | copy-start | bytes 1540
  53.4 2.4 %copy-start.75 = (f32[128]{0:T(128)}, f32[128]{0:T(128)S(1)}, u32[]{:S(2)}) copy-start(f32[128]{0:T(128)S(1)} %add_rsqrt_fusion.2) | copy-start | bytes 1540
  54.5 3.4 %copy-start.27 = (bf16[128,512]{1,0:T(8,128)(2,1)}, bf16[128,512]{1,0:T(8,128)(2,1)S(1)}, u32[]{:S(2)}) copy-start(bf16[128,512]{1,0:T(8,128)(2,1)S(1)} %fusion.12) | copy-start | bytes 393220
  54.5 3.4 %copy-start.10 = (bf16[128,512]{1,0:T(8,128)(2,1)S(1)}, bf16[128,512]{1,0:T(8,128)(2,1)}, u32[]{:S(2)}) copy-start(bf16[128,512]{1,0:T(8,128)(2,1)} %copy-done.9) | copy-start | bytes 393220
  65.2 3.0 %copy-start.19 = (f32[1024,512]{1,0:T(8,128)S(1)}, f32[1024,512]{1,0:T(8,128)}, u32[]{:S(2)}) copy-start(f32[1024,512]{1,0:T(8,128)} %copy-done.18) | copy-start | bytes 6291460
  65.2 3.1 %copy-start.83 = (bf16[2,512,512]{2,1,0:T(8,128)(2,1)S(1)}, bf16[2,512,512]{2,1,0:T(8,128)(2,1)}, u32[]{:S(2)}) copy-start(bf16[2,512,512]{2,1,0:T(8,128)(2,1)} %param.17) | copy-start | bytes 3145732
  69.6 3.5 %copy-start.28 = (bf16[1024,512]{1,0:T(8,128)(2,1)}, bf16[1024,512]{1,0:T(8,128)(2,1)S(1)}, u32[]{:S(2)}) copy-start(bf16[1024,512]{1,0:T(8,128)(2,1)S(1)} %multiply_convert_fusion.2) | copy-start | bytes 3145732
  69.6 1.6 copy-start.7
  71.2 2.6 %copy-start.11 = (bf16[128,512]{1,0:T(8,128)(2,1)S(1)}, bf16[128,512]{1,0:T(8,128)(2,1)}, u32[]{:S(2)}) copy-start(bf16[128,512]{1,0:T(8,128)(2,1)} %copy-done.9) | copy-start | bytes 393220
  71.2 3.7 %copy-start.72 = (bf16[512]{0:T(512)(128)(2,1)S(1)}, bf16[512]{0:T(512)(128)(2,1)}, u32[]{:S(2)}) copy-start(bf16[512]{0:T(512)(128)(2,1)} %get-tuple-element.16) | copy-start | bytes 3076
  71.2 3.8 %copy-start.77 = (bf16[512]{0:T(512)(128)(2,1)S(1)}, bf16[512]{0:T(512)(128)(2,1)}, u32[]{:S(2)}) copy-start(bf16[512]{0:T(512)(128)(2,1)} %get-tuple-element.8) | copy-start | bytes 3076
  73.1 2.7 %copy-start.42 = (bf16[512,512]{1,0:T(8,128)(2,1)}, bf16[512,512]{1,0:T(8,128)(2,1)S(1)}, u32[]{:S(2)}) copy-start(bf16[512,512]{1,0:T(8,128)(2,1)S(1)} %get-tuple-element.39) | copy-start | bytes 1572868
  75.8 12.3 %all-to-all-start.2 = ((bf16[8,32,512]{2,1,0:T(8,128)(2,1)}), bf16[8,32,512]{2,1,0:T(8,128)(2,1)}, u32[]{:S(2)}, u32[]{:S(2)}) async-start(bf16[8,32,512]{2,1,0:T(8,128)(2,1)} %bitcast.28), calls=%async_computation.2 | async-start | bytes 524288 | tf_op jit(solution)/shard_map/all_to_all | solution.py:54
  80.1 2.9 %copy-start.20 = (f32[1024,512]{1,0:T(8,128)S(1)}, f32[1024,512]{1,0:T(8,128)}, u32[]{:S(2)}) copy-start(f32[1024,512]{1,0:T(8,128)} %copy-done.18) | copy-start | bytes 6291460
  82.9 8.1 %copy-start.52 = (f32[1,512]{1,0:T(1,128)S(1)}, f32[1,512]{1,0:T(1,128)}, u32[]{:S(2)}) copy-start(f32[1,512]{1,0:T(1,128)} %get-tuple-element.27) | copy-start | bytes 6148
  88.1 5.0 %copy-start.14 = (f32[128,512]{1,0:T(8,128)S(1)}, f32[128,512]{1,0:T(8,128)}, u32[]{:S(2)}) copy-start(f32[128,512]{1,0:T(8,128)} %copy-done.13) | copy-start | bytes 786436
  88.1 5.0 %copy-start.57 = (f32[1,512]{1,0:T(1,128)S(1)}, f32[1,512]{1,0:T(1,128)}, u32[]{:S(2)}) copy-start(f32[1,512]{1,0:T(1,128)} %get-tuple-element.26) | copy-start | bytes 6148
  88.1 5.0 %copy-start.64 = (f32[128]{0:T(128)S(1)}, f32[128]{0:T(128)}, u32[]{:S(2)}) copy-start(f32[128]{0:T(128)} %copy-done.63) | copy-start | bytes 1540
  88.1 5.0 %copy-start.67 = (f32[128]{0:T(128)S(1)}, f32[128]{0:T(128)}, u32[]{:S(2)}) copy-start(f32[128]{0:T(128)} %copy-done.66) | copy-start | bytes 1540
  88.1 5.1 %copy-start.69 = (f32[128]{0:T(128)S(1)}, f32[128]{0:T(128)}, u32[]{:S(2)}) copy-start(f32[128]{0:T(128)} %copy-done.68) | copy-start | bytes 1540
  88.1 5.1 %copy-start.76 = (f32[128]{0:T(128)S(1)}, f32[128]{0:T(128)}, u32[]{:S(2)}) copy-start(f32[128]{0:T(128)} %copy-done.75) | copy-start | bytes 1540
  89.5 4.6 %copy-start.48 = (f32[128,512]{1,0:T(8,128)S(1)}, f32[128,512]{1,0:T(8,128)}, u32[]{:S(2)}) copy-start(f32[128,512]{1,0:T(8,128)} %copy-done.47) | copy-start | bytes 786436
  89.5 4.6 %copy-start.80 = (bf16[2,512,512]{2,1,0:T(8,128)(2,1)S(1)}, bf16[2,512,512]{2,1,0:T(8,128)(2,1)}, u32[]{:S(2)}) copy-start(bf16[2,512,512]{2,1,0:T(8,128)(2,1)} %param.19) | copy-start | bytes 3145732
  94.4 4.3 %copy-start.45 = (bf16[128,512]{1,0:T(8,128)(2,1)S(1)}, bf16[128,512]{1,0:T(8,128)(2,1)}, u32[]{:S(2)}) copy-start(bf16[128,512]{1,0:T(8,128)(2,1)} %copy-done.44) | copy-start | bytes 393220
  95.5 5.5 %copy-start.61 = (s32[1024]{0:T(1024)S(1)}, s32[1024]{0:T(1024)}, u32[]{:S(2)}) copy-start(s32[1024]{0:T(1024)} %param.23) | copy-start | bytes 12292
  98.7 5.4 %copy-start.50 = (f32[1,512]{1,0:T(1,128)S(1)}, f32[1,512]{1,0:T(1,128)}, u32[]{:S(2)}) copy-start(f32[1,512]{1,0:T(1,128)} %copy-done.49) | copy-start | bytes 6148
  107.5 1.6 copy-start.16
  107.5 1.8 copy-start.84
  109.3 1.6 copy-start.5
  112.5 3.6 %copy-start.71 = (bf16[512]{0:T(512)(128)(2,1)S(1)}, bf16[512]{0:T(512)(128)(2,1)}, u32[]{:S(2)}) copy-start(bf16[512]{0:T(512)(128)(2,1)} %get-tuple-element.14) | copy-start | bytes 3076
  112.5 8.0 %copy-start.21 = (bf16[512,512]{1,0:T(8,128)(2,1)S(1)}, bf16[512,512]{1,0:T(8,128)(2,1)}, u32[]{:S(2)}) copy-start(bf16[512,512]{1,0:T(8,128)(2,1)} %convolution_convert_fusion.5) | copy-start | bytes 1572868
  114.2 2.9 %copy-start.41 = (bf16[512,512]{1,0:T(8,128)(2,1)}, bf16[512,512]{1,0:T(8,128)(2,1)S(1)}, u32[]{:S(2)}) copy-start(bf16[512,512]{1,0:T(8,128)(2,1)S(1)} %get-tuple-element.43) | copy-start | bytes 1572868
  117.1 12.4 %all-to-all-start.3 = ((bf16[8,32,512]{2,1,0:T(8,128)(2,1)}), bf16[8,32,512]{2,1,0:T(8,128)(2,1)S(1)}, u32[]{:S(2)}, u32[]{:S(2)}) async-start(bf16[8,32,512]{2,1,0:T(8,128)(2,1)} %bitcast.30), calls=%async_computation.3 | async-start | bytes 524288 | tf_op jit(solution)/shard_map/all_to_all | solution.py:54
  123.9 2.4 %copy-start.22 = (bf16[512,512]{1,0:T(8,128)(2,1)S(1)}, bf16[512,512]{1,0:T(8,128)(2,1)}, u32[]{:S(2)}) copy-start(bf16[512,512]{1,0:T(8,128)(2,1)} %convolution_convert_fusion.9) | copy-start | bytes 1572868
  123.9 2.4 %copy-start.23 = (bf16[512,512]{1,0:T(8,128)(2,1)S(1)}, bf16[512,512]{1,0:T(8,128)(2,1)}, u32[]{:S(2)}) copy-start(bf16[512,512]{1,0:T(8,128)(2,1)} %fusion.5) | copy-start | bytes 1572868
  123.9 2.5 %copy-start.30 = (bf16[1024,512]{0,1:T(8,128)(2,1)S(1)}, bf16[1024,512]{0,1:T(8,128)(2,1)}, u32[]{:S(2)}) copy-start(bf16[1024,512]{0,1:T(8,128)(2,1)} %copy-done.29) | copy-start | bytes 3145732
  126.3 1.6 copy-start.17
  127.8 1.6 copy-start.55
  135.0 68.4 %copy-start.36 = (f32[128,512]{1,0:T(8,128)S(1)}, f32[128,512]{1,0:T(8,128)}, u32[]{:S(2)}) copy-start(f32[128,512]{1,0:T(8,128)} %convolution_add_fusion.5) | copy-start | bytes 786436
  (25 other events, 28.8 us)
